TPU v7x, 256 devices: a whole 4x4x8 slice. The times are simulated.
256 devices in a mesh: chain: 128 (over y_lo, x, z, core), shard: 2 (over y_hi).
Axes of the slice: x: 4, y: 4 (y_hi: 2, y_lo: 2; y = y_hi * 2 + y_lo), z: 8, core: 2. Of those that a mesh axis runs over, the one named last changes fastest.
Arguments:
- w_pair: bfloat16 [128, 2, 256, 4096], P('chain', None, 'shard'), may hold values from -6 to 6
- w_down: bfloat16 [128, 256, 4096], P('chain', 'shard'), may hold values from -6 to 6
- tokens: bfloat16 [128, 512, 4096], P('chain', 'shard'), may hold values from -6 to 6
- cotangent: bfloat16 [128, 512, 4096], P('chain', 'shard'), may hold values from -6 to 6
- seq_ids: int32 [128, 512], P('chain', 'shard'), may hold values from 0 to 7, never falling along the last dimension, each value on 1 to 128 neighbouring positions
- msg_left: bfloat16 [128, 2, 256, 4096], P('chain', None, 'shard'), may hold values from -9 to 9
- msg_right: bfloat16 [128, 2, 256, 4096], P('chain', None, 'shard'), may hold values from -9 to 9
- count_left: int32 [128], P('chain'), may hold values from 0 to 5, as said below
- count_right: int32 [128], P('chain'), may hold values from 0 to 5, as said below
Outputs:
- new_pair: bfloat16 [128, 2, 256, 4096], P('chain', None, 'shard')
Inputs may be any that keep to these rules, and one draw needn't show every extreme that they name: count_left of worker w is at most min(w, 5); some worker at least 5 from both ends of the chain has count_left equal to 5. count_right of worker w is at most min(127 - w, 5); the same worker has count_right equal to 5.
All inputs are finite; a program needn't handle non-finite values.
Results may differ from a plain program's by a relative error of at most 0.0053.
Values may be sent and summed in bfloat16 or wider, within the bound.
A program may use at most 128 MiB of HBM per device.

v0:
```python
import math

import jax
import jax.numpy as jnp
from jax import lax
from jax.sharding import PartitionSpec as P

D = 4096
SEQS = 8


learn_rate = 1.0


def from_everyone(shard, axis):
    copies = jnp.broadcast_to(shard, (lax.axis_size(axis), *shard.shape))
    return lax.all_to_all(copies, axis, split_axis=0, concat_axis=0, tiled=True)


def laid_out(pieces, dim):
    pieces = jnp.moveaxis(pieces, 0, dim)
    shape = pieces.shape
    return pieces.reshape(*shape[:dim], shape[dim] * shape[dim + 1], *shape[dim + 2 :])


def gather_directly(shard, axis, dim):
    pieces = from_everyone(shard, axis)
    return laid_out(pieces, dim)


def side_by_side(arrays, axis, dim, along):
    widths = [math.prod(a.shape[along:]) for a in arrays]
    both = jnp.concatenate(
        [a.reshape(*a.shape[:along], w) for a, w in zip(arrays, widths)], axis=along
    )
    filled = gather_directly(both, axis, dim)
    pieces = jnp.split(filled, [sum(widths[:k]) for k in range(1, len(widths))], axis=along)
    return tuple(
        (b.reshape(*filled.shape[:along], *a.shape[along:]) for a, b in zip(arrays, pieces))
    )


def passed_along(shard, axis, by):
    peers = lax.axis_size(axis)
    pairs = [(i, i + by) for i in range(peers) if 0 <= i + by < peers]
    return lax.ppermute(shard, axis, pairs)


def body(w_pair, w_down, tokens, cotangent, seq_ids, msg_left, msg_right, count_left, count_right):
    tok_rows, cot_rows, id_wire = side_by_side(
        (tokens[0], cotangent[0], seq_ids[0].astype(jnp.bfloat16)), "shard", 0, 1
    )
    segment_ids = id_wire.astype(jnp.int32)
    total_rows = tok_rows.shape[0]
    width_scale = D ** (-0.5)
    pair_local = w_pair[0]
    contract_last = (((1,), (1,)), ((), ()))
    gate_pre = (
        lax.dot_general(tok_rows, pair_local[0], contract_last, preferred_element_type=jnp.float32)
        * width_scale
    )
    up_pre = (
        lax.dot_general(tok_rows, pair_local[1], contract_last, preferred_element_type=jnp.float32)
        * width_scale
    )
    one_hot = (segment_ids[:, None] == jnp.arange(SEQS, dtype=jnp.int32)[None, :]).astype(
        jnp.float32
    )
    seq_count = jnp.sum(one_hot, axis=0)
    seq_len = jnp.sum(one_hot * seq_count[None, :], axis=1)
    tok_weight = total_rows / SEQS / seq_len
    scaled_cot = (tok_weight[:, None] * cot_rows.astype(jnp.float32)).astype(jnp.bfloat16)
    grad_hidden = (
        lax.dot_general(scaled_cot, w_down[0], contract_last, preferred_element_type=jnp.float32)
        * width_scale
    )
    sigmoid_gate = jax.nn.sigmoid(gate_pre)
    grad_gate = (
        grad_hidden * up_pre * sigmoid_gate * (1.0 + gate_pre * (1.0 - sigmoid_gate))
    ).astype(jnp.bfloat16)
    grad_up = (grad_hidden * gate_pre * sigmoid_gate).astype(jnp.bfloat16)
    batch_scale = total_rows ** (-0.5)
    contract_tokens = (((0,), (0,)), ((), ()))
    out_right_count = (1 + count_left).astype(jnp.bfloat16)
    out_left_count = (1 + count_right).astype(jnp.bfloat16)
    gate_part = lax.dot_general(
        grad_gate, tok_rows, contract_tokens, preferred_element_type=jnp.float32
    )
    up_part = lax.dot_general(
        grad_up, tok_rows, contract_tokens, preferred_element_type=jnp.float32
    )
    half_step = pair_local.astype(jnp.float32) - learn_rate * (
        jnp.stack([gate_part, up_part]) * batch_scale
    )
    send_right = (half_step + msg_left[0].astype(jnp.float32)).astype(jnp.bfloat16)
    send_left = (half_step + msg_right[0].astype(jnp.float32)).astype(jnp.bfloat16)
    recv_left, cnt_left = passed_along((send_right, out_right_count), "chain", 1)
    recv_right, cnt_right = passed_along((send_left, out_left_count), "chain", -1)
    total_count = 1.0 + cnt_left.astype(jnp.float32) + cnt_right.astype(jnp.float32)
    updated = (
        half_step + recv_left.astype(jnp.float32) + recv_right.astype(jnp.float32)
    ) / total_count
    return updated.astype(jnp.bfloat16)[None]


def solution(mesh):
    return jax.shard_map(
        body,
        mesh=mesh,
        in_specs=(
            P("chain", None, "shard", None),
            P("chain", "shard", None),
            P("chain", "shard", None),
            P("chain", "shard", None),
            P("chain", "shard"),
            P("chain", None, "shard", None),
            P("chain", None, "shard", None),
            P("chain"),
            P("chain"),
        ),
        out_specs=P("chain", None, "shard", None),
        check_vma=False,
    )
```

profile of v0, /device:TPU:99, one launch (start us, length us, event | category | flops | bytes accessed | tf_op | source)
XLA Modules:
  0.0 184.9 jit_solution(14382709713788557498)
XLA Ops:
  0.0 0.0 copy-start
  0.0 0.8 convert_bitcast_fusion
  0.8 0.1 copy.17
  0.9 3.7 %pad_maximum_fusion = bf16[256,8193]{1,0:T(8,128)(2,1)} fusion(bf16[256,1]{1,0:T(8,128)(2,1)S(1)} %copy.17, bf16[256,4096]{1,0:T(8,128)(2,1)} %bitcast.42, bf16[256,4096]{1,0:T(8,128)(2,1)} %bitcast.43), kind=kLoop, calls=%fused_computation.3 | loop fusion | flops 12584448 | bytes 8389632 | tf_op jit(solution)/shard_map/concatenate | solution.py:33
  4.6 6.4 %copy.18 = bf16[256,8193]{0,1:T(8,128)(2,1)} copy(bf16[256,8193]{1,0:T(8,128)(2,1)} %pad_maximum_fusion) | data formatting | bytes 8389632 | tf_op jit(solution)/shard_map/concatenate | solution.py:33
  11.0 3.4 %broadcast_in_dim.4 = bf16[2,256,8193]{1,2,0:T(8,128)(2,1)S(1)} broadcast(bf16[256,8193]{0,1:T(8,128)(2,1)} %copy.18), dimensions={1,2} | broadcast | bytes 12584448 | tf_op jit(solution)/shard_map/broadcast_in_dim | solution.py:16
  14.5 97.7 %all_to_all.5 = bf16[2,256,8193]{1,2,0:T(8,128)(2,1)} all-to-all(bf16[2,256,8193]{1,2,0:T(8,128)(2,1)S(1)} %broadcast_in_dim.4), channel_id=1, replica_groups=mesh['chain'=128,'shard'=2] {'shard'}, dimensions={0} | all-to-all | bytes 16779264 | tf_op jit(solution)/shard_map/all_to_all | solution.py:17
  112.1 0.0 copy-start.2
  112.1 12.0 %copy.19 = bf16[2,256,8193]{2,1,0:T(8,128)(2,1)} copy(bf16[2,256,8193]{1,2,0:T(8,128)(2,1)} %all_to_all.5) | data formatting | bytes 16779264 | tf_op jit(solution)/shard_map/all_to_all | solution.py:17
  124.1 1.1 convert_reduce_fusion
  125.1 0.1 convert_reduce_fusion.1
  125.3 0.1 select_reduce_fusion
  125.3 0.0 copy-done.2
  125.4 0.0 copy-start.1
  125.4 3.6 %fusion.17 = f32[512,128]{1,0:T(8,128)S(1)} fusion(bf16[512,8193]{1,0:T(8,128)(2,1)} %bitcast.38, bf16[1,2,128,4096]{3,2,1,0:T(8,128)(2,1)S(1)} %copy-done.2), kind=kOutput, calls=%fused_computation.23 | convolution fusion | flops 536936448 | bytes 5505024 | tf_op jit(solution)/shard_map/dot_general | solution.py:59
  129.0 0.0 copy-done
  129.0 1.1 copy-done.1
  130.0 2.1 %fusion.13 = f32[512,128]{1,0:T(8,128)} fusion(bf16[512,8193]{1,0:T(8,128)(2,1)S(1)} %bitcast.41, f32[512]{0:T(512)S(1)} %broadcast_divide_fusion, bf16[1,128,4096]{2,1,0:T(8,128)(2,1)S(1)} %copy-done), kind=kOutput, calls=%fused_computation.21 | convolution fusion | flops 543227904 | bytes 5507072 | tf_op jit(solution)/shard_map/dot_general | solution.py:74
  132.1 8.0 %convolution_bitcast_fusion.1 = f32[1,128,4096]{2,1,0:T(8,128)} fusion(bf16[512,8193]{1,0:T(8,128)(2,1)} %bitcast.39, f32[512,128]{1,0:T(8,128)} %fusion.13, bf16[1,2,128,4096]{3,2,1,0:T(8,128)(2,1)S(1)} %copy-done.2, f32[512,128]{1,0:T(8,128)S(1)} %fusion.17), kind=kOutput, calls=%fused_computation.2 | convolution fusion | flops 1074462720 | bytes 12058624 | tf_op jit(solution)/shard_map/dot_general | solution.py:86
  140.1 3.2 %convolution_bitcast_fusion = f32[1,128,4096]{2,1,0:T(8,128)S(1)} fusion(bf16[512,8193]{1,0:T(8,128)(2,1)} %bitcast.40, f32[512,128]{1,0:T(8,128)} %fusion.13, f32[512,128]{1,0:T(8,128)S(1)} %fusion.17), kind=kOutput, calls=%fused_computation.1 | convolution fusion | flops 537264128 | bytes 6815744 | tf_op jit(solution)/shard_map/dot_general | solution.py:89
  143.3 0.0 copy-done.3
  143.3 0.3 copy-done.4
  143.7 0.6 copy-done.5
  144.3 1.5 fusion.4
  145.9 6.2 %collective-permute-start = (bf16[2,128,4096]{2,1,0:T(8,128)(2,1)S(1)}, bf16[2,128,4096]{2,1,0:T(8,128)(2,1)S(1)}, u32[]{:S(2)}, u32[]{:S(2)}) collective-permute-start(bf16[2,128,4096]{2,1,0:T(8,128)(2,1)S(1)} %get-tuple-element.5), channel_id=1, source_target_pairs={{0,2},{2,4},{4,6},{6,8},{8,10},{10,12},{12,14},{14,16},{16,18},{18... | collective-permute-start | bytes 6291464 | tf_op jit(solution)/shard_map/ppermute | solution.py:46
  152.0 1.9 %collective-permute-start.1 = (bf16[2,128,4096]{2,1,0:T(8,128)(2,1)S(1)}, bf16[2,128,4096]{2,1,0:T(8,128)(2,1)S(1)}, u32[]{:S(2)}, u32[]{:S(2)}) collective-permute-start(bf16[2,128,4096]{2,1,0:T(8,128)(2,1)S(1)} %get-tuple-element.6), channel_id=1, source_target_pairs={{2,0},{4,2},{6,4},{8,6},{10,8},{12,10},{14,12},{16,14},{18,16},{20... | collective-permute-start | bytes 6291464 | tf_op jit(solution)/shard_map/ppermute | solution.py:46
  154.6 20.4 %collective-permute-start.2 = (bf16[1]{0:T(256)(128)(2,1)}, bf16[1]{0:T(256)(128)(2,1)}, u32[]{:S(2)}, u32[]{:S(2)}) collective-permute-start(bf16[1]{0:T(256)(128)(2,1)} %convert_element_type.92), channel_id=1, source_target_pairs={{0,2},{2,4},{4,6},{6,8},{8,10},{10,12},{12,14},{14,16},{16,18},{18... | collective-permute-start | bytes 14 | tf_op jit(solution)/shard_map/ppermute | solution.py:46
  175.7 2.7 %collective-permute-start.3 = (bf16[1]{0:T(256)(128)(2,1)}, bf16[1]{0:T(256)(128)(2,1)}, u32[]{:S(2)}, u32[]{:S(2)}) collective-permute-start(bf16[1]{0:T(256)(128)(2,1)} %convert_element_type.94), channel_id=1, source_target_pairs={{2,0},{4,2},{6,4},{8,6},{10,8},{12,10},{14,12},{16,14},{18,16},{20... | collective-permute-start | bytes 14 | tf_op jit(solution)/shard_map/ppermute | solution.py:46
  179.0 2.9 %collective-permute-done.3 = bf16[1]{0:T(256)(128)(2,1)} collective-permute-done((bf16[1]{0:T(256)(128)(2,1)}, bf16[1]{0:T(256)(128)(2,1)}, u32[]{:S(2)}, u32[]{:S(2)}) %collective-permute-start.3) | collective-permute-done | bytes 34 | tf_op jit(solution)/shard_map/ppermute | solution.py:46
  182.5 0.0 collective-permute-done
  182.6 0.0 collective-permute-done.1
  182.6 2.3 %fusion.12 = bf16[1,2,128,4096]{3,2,1,0:T(8,128)(2,1)} fusion(f32[]{:T(128)} %bitcast.12, bf16[2,128,4096]{2,1,0:T(8,128)(2,1)S(1)} %collective-permute-done.1, bf16[2,128,4096]{2,1,0:T(8,128)(2,1)S(1)} %collective-permute-done, f32[1,128,4096]{2,1,0:T(8,128)S(1)} %convolution_bitcast_fusion, f32[1,128,4096]{2,1,0:T(8,128)S(1)} %copy-done.3, ...), kind=kLoop, calls=%fused_computation.20 | loop fusion | flops 10485760 | bytes 12582916 | tf_op jit(solution)/shard_map/broadcast_in_dim | solution.py:103
  (5 shorter events, 0.0 us)
Async XLA Ops:
  0.0 129.0 %copy-start = (bf16[1,128,4096]{2,1,0:T(8,128)(2,1)S(1)}, bf16[1,128,4096]{2,1,0:T(8,128)(2,1)}, u32[]{:S(2)}) copy-start(bf16[1,128,4096]{2,1,0:T(8,128)(2,1)} %param.10) | copy-start | bytes 3145732
  112.1 13.2 %copy-start.2 = (bf16[1,2,128,4096]{3,2,1,0:T(8,128)(2,1)S(1)}, bf16[1,2,128,4096]{3,2,1,0:T(8,128)(2,1)}, u32[]{:S(2)}) copy-start(bf16[1,2,128,4096]{3,2,1,0:T(8,128)(2,1)} %param.9) | copy-start | bytes 6291460
  125.4 4.7 %copy-start.1 = (bf16[2,256,8193]{2,1,0:T(8,128)(2,1)S(1)}, bf16[2,256,8193]{2,1,0:T(8,128)(2,1)}, u32[]{:S(2)}) copy-start(bf16[2,256,8193]{2,1,0:T(8,128)(2,1)} %copy.19) | copy-start | bytes 25168900
  140.1 3.2 %copy-start.3 = (f32[1,128,4096]{2,1,0:T(8,128)S(1)}, f32[1,128,4096]{2,1,0:T(8,128)}, u32[]{:S(2)}) copy-start(f32[1,128,4096]{2,1,0:T(8,128)} %convolution_bitcast_fusion.1) | copy-start | bytes 6291460
  140.1 3.6 %copy-start.4 = (bf16[1,2,128,4096]{3,2,1,0:T(8,128)(2,1)S(1)}, bf16[1,2,128,4096]{3,2,1,0:T(8,128)(2,1)}, u32[]{:S(2)}) copy-start(bf16[1,2,128,4096]{3,2,1,0:T(8,128)(2,1)} %param.14) | copy-start | bytes 6291460
  140.1 4.2 %copy-start.5 = (bf16[1,2,128,4096]{3,2,1,0:T(8,128)(2,1)S(1)}, bf16[1,2,128,4096]{3,2,1,0:T(8,128)(2,1)}, u32[]{:S(2)}) copy-start(bf16[1,2,128,4096]{3,2,1,0:T(8,128)(2,1)} %param.15) | copy-start | bytes 6291460
  145.9 36.7 %collective-permute-start = (bf16[2,128,4096]{2,1,0:T(8,128)(2,1)S(1)}, bf16[2,128,4096]{2,1,0:T(8,128)(2,1)S(1)}, u32[]{:S(2)}, u32[]{:S(2)}) collective-permute-start(bf16[2,128,4096]{2,1,0:T(8,128)(2,1)S(1)} %get-tuple-element.5), channel_id=1, source_target_pairs={{0,2},{2,4},{4,6},{6,8},{8,10},{10,12},{12,14},{14,16},{16,18},{18... | collective-permute-start | bytes 6291464 | tf_op jit(solution)/shard_map/ppermute | solution.py:46
  152.0 30.5 %collective-permute-start.1 = (bf16[2,128,4096]{2,1,0:T(8,128)(2,1)S(1)}, bf16[2,128,4096]{2,1,0:T(8,128)(2,1)S(1)}, u32[]{:S(2)}, u32[]{:S(2)}) collective-permute-start(bf16[2,128,4096]{2,1,0:T(8,128)(2,1)S(1)} %get-tuple-element.6), channel_id=1, source_target_pairs={{2,0},{4,2},{6,4},{8,6},{10,8},{12,10},{14,12},{16,14},{18,16},{20... | collective-permute-start | bytes 6291464 | tf_op jit(solution)/shard_map/ppermute | solution.py:46
  154.6 23.8 %collective-permute-start.2 = (bf16[1]{0:T(256)(128)(2,1)}, bf16[1]{0:T(256)(128)(2,1)}, u32[]{:S(2)}, u32[]{:S(2)}) collective-permute-start(bf16[1]{0:T(256)(128)(2,1)} %convert_element_type.92), channel_id=1, source_target_pairs={{0,2},{2,4},{4,6},{6,8},{8,10},{10,12},{12,14},{14,16},{16,18},{18... | collective-permute-start | bytes 14 | tf_op jit(solution)/shard_map/ppermute | solution.py:46
  175.7 6.2 %collective-permute-start.3 = (bf16[1]{0:T(256)(128)(2,1)}, bf16[1]{0:T(256)(128)(2,1)}, u32[]{:S(2)}, u32[]{:S(2)}) collective-permute-start(bf16[1]{0:T(256)(128)(2,1)} %convert_element_type.94), channel_id=1, source_target_pairs={{2,0},{4,2},{6,4},{8,6},{10,8},{12,10},{14,12},{16,14},{18,16},{20... | collective-permute-start | bytes 14 | tf_op jit(solution)/shard_map/ppermute | solution.py:46
where the time goes:
time: 186 us; the launch traced here: 185 us
  blocking collectives  97.7 us (53%)
  starting transfers between devices  31.2 us (17%)
  local copies, waits for them, and re-layouts  24 us (13%)
  matrix products  16.9 us (9%)
  other arithmetic  9.52 us (5%)
  waiting for transfers between devices  2.86 us (2%)
  between operations  2.67 us (1%)
    all_to_all x1, blocking collectives, from_everyone(): return lax.all_to_all(copies, axis, split_axis=0, concat_axis=0, tiled=True)  97.7 us
    ppermute x4, starting transfers between devices, passed_along(): return lax.ppermute(shard, axis, pairs)  31.2 us
    all_to_all x1, local copies, waits for them, and re-layouts, from_everyone(): return lax.all_to_all(copies, axis, split_axis=0, concat_axis=0, tiled=True)  12 us
    dot_general x1, matrix products, body(): lax.dot_general(grad_gate, tok_rows, contract_tokens, preferred_element_t...  7.99 us
    concatenate x1, local copies, waits for them, and re-layouts, side_by_side(): jnp.concatenate([a.reshape(*a.shape[:along], w) for a, w in zip(arrays, w...  6.44 us
  transfers between devices with their start and end apart: 4, of which 1 were waited for; matrix products, arithmetic and copies ran while one was open for 0% of the time, Pallas kernels for 0%

commit v1 on v0

v1 whole, which is shorter than its diff:
```python
import functools

import jax
import jax.numpy as jnp
from jax import lax
from jax.experimental import pallas as pl
from jax.experimental.pallas import tpu as pltpu
from jax.sharding import PartitionSpec as P

MESH = pl.DeviceIdType.MESH
F32 = jnp.float32
BF16 = jnp.bfloat16
learn_rate = 1.0
SEQS = 8

CHUNKS = ((0, 32), (32, 32), (64, 32), (96, 16), (112, 16))
TILE = 512


def dot_nt(a, b):
    return lax.dot_general(a, b, (((1,), (1,)), ((), ())), preferred_element_type=F32)


def gate_factors(pre, hidden):
    gate, up = pre[:hidden], pre[hidden:]
    sig = jax.nn.sigmoid(gate)
    return up * sig * (1.0 + gate * (1.0 - sig)), gate * sig


def kernel(
    workers,
    w_pair,
    w_down,
    tokens,
    cotangent,
    seq_ids,
    msg_left,
    msg_right,
    count_left,
    count_right,
    out,
    wp,
    wd,
    tok,
    cot,
    ids,
    ml,
    mr,
    cl,
    cr,
    tok_p,
    wd_p,
    ids_p,
    gh_out,
    gh_p,
    fac_gate,
    fac_up,
    lhs,
    weight,
    half,
    send_r,
    send_l,
    recv_l,
    recv_r,
    cnt_r_out,
    cnt_l_out,
    cnt_l,
    cnt_r,
    new,
    load_sem,
    out_sem,
    y_send,
    y_recv,
    wd_send,
    wd_recv,
    gh_send,
    gh_recv,
    r_send,
    r_recv,
    l_send,
    l_recv,
):
    me, side = lax.axis_index("chain"), lax.axis_index("shard")
    partner = (me, 1 - side)
    last = workers - 1
    right, left = ((me + 1) % workers, side), ((me + last) % workers, side)
    has_left, has_right = me > 0, me < last
    rows, width = tok.shape
    hidden = wd.shape[0]
    width_scale = width**-0.5
    batch_scale = (2 * rows) ** -0.5
    n = len(CHUNKS)
    tiles = width // TILE

    def remote(src, dst, send, recv, device):
        return pltpu.make_async_remote_copy(
            src_ref=src, dst_ref=dst, send_sem=send, recv_sem=recv, device_id=device, device_id_type=MESH
        )

    def cols(j):
        return pl.ds(pl.multiple_of(j * TILE, TILE), TILE)

    barrier = pltpu.get_barrier_semaphore()
    pl.semaphore_signal(barrier, inc=1, device_id=partner, device_id_type=MESH)

    @pl.when(has_left)
    def _():
        pl.semaphore_signal(barrier, inc=1, device_id=left, device_id_type=MESH)

    @pl.when(has_right)
    def _():
        pl.semaphore_signal(barrier, inc=1, device_id=right, device_id_type=MESH)

    loads = [
        pltpu.make_async_copy(src, dst, load_sem.at[k])
        for k, (src, dst) in enumerate(
            (
                (tokens.at[0], tok),
                (w_pair.at[0], wp),
                (cotangent.at[0], cot),
                (w_down.at[0], wd),
                (seq_ids, ids),
                (msg_left.at[0], ml),
                (msg_right.at[0], mr),
                (count_left, cl),
                (count_right, cr),
            )
        )
    ]
    for load in loads:
        load.start()

    pl.semaphore_wait(barrier, 1 + has_left.astype(jnp.int32) + has_right.astype(jnp.int32))

    ids_copy = remote(seq_ids, ids_p, y_send.at[0], y_recv.at[0], partner)
    tok_copy = remote(tokens.at[0], tok_p, y_send.at[1], y_recv.at[1], partner)
    wd_copies = [
        remote(
            w_down.at[0, pl.ds(r0, r)], wd_p.at[pl.ds(r0, r)], wd_send.at[c], wd_recv.at[c], partner
        )
        for c, (r0, r) in enumerate(CHUNKS)
    ]
    gh_copies = [
        remote(gh_out.at[pl.ds(r0, r)], gh_p.at[pl.ds(r0, r)], gh_send.at[c], gh_recv.at[c], partner)
        for c, (r0, r) in enumerate(CHUNKS)
    ]
    r_copies = [
        remote(
            send_r.at[:, pl.ds(r0, r)], recv_l.at[:, pl.ds(r0, r)], r_send.at[c], r_recv.at[c], right
        )
        for c, (r0, r) in enumerate(CHUNKS)
    ] + [remote(cnt_r_out, cnt_l, r_send.at[n], r_recv.at[n], right)]
    l_copies = [
        remote(
            send_l.at[:, pl.ds(r0, r)], recv_r.at[:, pl.ds(r0, r)], l_send.at[c], l_recv.at[c], left
        )
        for c, (r0, r) in enumerate(CHUNKS)
    ] + [remote(cnt_l_out, cnt_r, l_send.at[n], l_recv.at[n], left)]
    out_copies = [
        pltpu.make_async_copy(
            new.at[:, pl.ds(r0, r)], out.at[0, :, pl.ds(r0, r)], out_sem.at[c]
        )
        for c, (r0, r) in enumerate(CHUNKS)
    ]

    def send_chain(c):
        @pl.when(has_right)
        def _():
            r_copies[c].start()

        @pl.when(has_left)
        def _():
            l_copies[c].start()

    ids_copy.start()
    wd_copies[0].start()
    tok_copy.start()

    @pl.when(jnp.logical_not(has_left))
    def _():
        recv_l[...] = jnp.zeros_like(recv_l)
        cnt_l[...] = jnp.zeros_like(cnt_l)

    @pl.when(jnp.logical_not(has_right))
    def _():
        recv_r[...] = jnp.zeros_like(recv_r)
        cnt_r[...] = jnp.zeros_like(cnt_r)

    loads[0].wait()
    loads[1].wait()
    w_all = wp[...].reshape(2 * hidden, width)
    gate_own, up_own = gate_factors(dot_nt(w_all, tok[...]) * width_scale, hidden)

    loads[4].wait()
    ids_copy.wait_recv()
    own_row = ids[...]
    shape = (rows, rows)
    diag = lax.broadcasted_iota(jnp.int32, shape, 0) == lax.broadcasted_iota(jnp.int32, shape, 1)
    own_col = jnp.sum(jnp.where(diag, own_row, 0), axis=1, keepdims=True)
    peer_col = jnp.sum(jnp.where(diag, ids_p[...], 0), axis=1, keepdims=True)
    seq_len = jnp.sum((own_col == own_row).astype(F32), axis=0, keepdims=True) + jnp.sum(
        (peer_col == own_row).astype(F32), axis=0, keepdims=True
    )
    weight[...] = (2 * rows / SEQS) / seq_len * width_scale

    loads[2].wait()
    loads[3].wait()
    gh_own = dot_nt(wd[...], cot[...]) * weight[...]
    lhs[:hidden] = (gh_own * gate_own).astype(BF16)
    lhs[hidden:] = (gh_own * up_own).astype(BF16)

    def own_tile(j, carry):
        part = jnp.dot(lhs[...], tok[:, cols(j)], preferred_element_type=F32)
        part = part.reshape(2, hidden, TILE) * (learn_rate * batch_scale)
        half[:, :, cols(j)] = wp[:, :, cols(j)].astype(F32) - part
        return carry

    lax.fori_loop(0, tiles, own_tile, 0)

    def partner_grad_hidden(c):
        r0, r = CHUNKS[c]
        wd_copies[c].wait_recv()
        gh = dot_nt(wd_p[r0 : r0 + r], cot[...]) * weight[...]
        gh_out[r0 : r0 + r] = gh.astype(BF16)
        gh_copies[c].start()

    def finish_rows(c):
        r0, r = CHUNKS[c]
        gh_copies[c].wait_recv()
        gh = gh_p[r0 : r0 + r].astype(F32)
        both = jnp.concatenate(
            [gh * fac_gate[r0 : r0 + r], gh * fac_up[r0 : r0 + r]], axis=0
        ).astype(BF16)

        def tile(j, carry):
            part = jnp.dot(both, tok_p[:, cols(j)], preferred_element_type=F32)
            part = part.reshape(2, r, TILE) * (learn_rate * batch_scale)
            step = half[:, r0 : r0 + r, cols(j)] - part
            half[:, r0 : r0 + r, cols(j)] = step
            send_r[:, r0 : r0 + r, cols(j)] = (
                step + ml[:, r0 : r0 + r, cols(j)].astype(F32)
            ).astype(BF16)
            send_l[:, r0 : r0 + r, cols(j)] = (
                step + mr[:, r0 : r0 + r, cols(j)].astype(F32)
            ).astype(BF16)
            return carry

        lax.fori_loop(0, tiles, tile, 0)
        send_chain(c)

    partner_grad_hidden(0)
    for c in range(1, min(3, n)):
        wd_copies[c].start()

    for k in (5, 6, 7, 8):
        loads[k].wait()
    cnt_r_out[...] = jnp.full(cnt_r_out.shape, 1 + cl[0], jnp.int32)
    cnt_l_out[...] = jnp.full(cnt_l_out.shape, 1 + cr[0], jnp.int32)
    send_chain(n)

    tok_copy.wait_recv()
    gate_peer, up_peer = gate_factors(dot_nt(w_all, tok_p[...]) * width_scale, hidden)
    fac_gate[...] = gate_peer
    fac_up[...] = up_peer
    finish_rows(0)
    for c in range(1, n):
        partner_grad_hidden(c)
        if c + 2 < n:
            wd_copies[c + 2].start()
        if c >= 2:
            finish_rows(c - 1)
    finish_rows(n - 1)

    @pl.when(has_left)
    def _():
        r_copies[n].wait_recv()

    @pl.when(has_right)
    def _():
        l_copies[n].wait_recv()

    inverse = 1.0 / (1.0 + cnt_l[...].astype(F32) + cnt_r[...].astype(F32))

    for c, (r0, r) in enumerate(CHUNKS):

        @pl.when(has_left)
        def _(c=c):
            r_copies[c].wait_recv()

        @pl.when(has_right)
        def _(c=c):
            l_copies[c].wait_recv()

        def tile(j, carry, r0=r0, r=r):
            total = (
                half[:, r0 : r0 + r, cols(j)]
                + recv_l[:, r0 : r0 + r, cols(j)].astype(F32)
                + recv_r[:, r0 : r0 + r, cols(j)].astype(F32)
            )
            new[:, r0 : r0 + r, cols(j)] = (total * inverse.reshape(1, 1, TILE)).astype(BF16)
            return carry

        lax.fori_loop(0, tiles, tile, 0)
        out_copies[c].start()

    ids_copy.wait_send()
    tok_copy.wait_send()
    for c in range(n):
        wd_copies[c].wait_send()
        gh_copies[c].wait_send()
    for c in range(n + 1):

        @pl.when(has_right)
        def _(c=c):
            r_copies[c].wait_send()

        @pl.when(has_left)
        def _(c=c):
            l_copies[c].wait_send()

    for copy in out_copies:
        copy.wait()


def body(w_pair, w_down, tokens, cotangent, seq_ids, msg_left, msg_right, count_left, count_right):
    workers = lax.axis_size("chain")
    pair = w_pair.shape[1:]
    hidden, width = pair[1:]
    rows = tokens.shape[1]
    n = len(CHUNKS)
    any_space = pl.BlockSpec(memory_space=pltpu.HBM)
    vm, dma = pltpu.VMEM, pltpu.SemaphoreType.DMA
    return pl.pallas_call(
        functools.partial(kernel, workers),
        out_shape=jax.ShapeDtypeStruct(w_pair.shape, BF16),
        in_specs=[any_space] * 9,
        out_specs=any_space,
        scratch_shapes=[
            vm(pair, BF16),
            vm((hidden, width), BF16),
            vm((rows, width), BF16),
            vm((rows, width), BF16),
            vm((1, rows), jnp.int32),
            vm(pair, BF16),
            vm(pair, BF16),
            pltpu.SMEM((1,), jnp.int32),
            pltpu.SMEM((1,), jnp.int32),
            vm((rows, width), BF16),
            vm((hidden, width), BF16),
            vm((1, rows), jnp.int32),
            vm((hidden, rows), BF16),
            vm((hidden, rows), BF16),
            vm((hidden, rows), F32),
            vm((hidden, rows), F32),
            vm((2 * hidden, rows), BF16),
            vm((1, rows), F32),
            vm(pair, F32),
            vm(pair, BF16),
            vm(pair, BF16),
            vm(pair, BF16),
            vm(pair, BF16),
            vm((1, TILE), jnp.int32),
            vm((1, TILE), jnp.int32),
            vm((1, TILE), jnp.int32),
            vm((1, TILE), jnp.int32),
            vm(pair, BF16),
            dma((9,)),
            dma((n,)),
            dma((2,)),
            dma((2,)),
            dma((n,)),
            dma((n,)),
            dma((n,)),
            dma((n,)),
            dma((n + 1,)),
            dma((n + 1,)),
            dma((n + 1,)),
            dma((n + 1,)),
        ],
        compiler_params=pltpu.CompilerParams(
            collective_id=0, has_side_effects=True, vmem_limit_bytes=60 * 1024 * 1024
        ),
    )(w_pair, w_down, tokens, cotangent, seq_ids, msg_left, msg_right, count_left, count_right)


def solution(mesh):
    return jax.shard_map(
        body,
        mesh=mesh,
        in_specs=(
            P("chain", None, "shard", None),
            P("chain", "shard", None),
            P("chain", "shard", None),
            P("chain", "shard", None),
            P("chain", "shard"),
            P("chain", None, "shard", None),
            P("chain", None, "shard", None),
            P("chain"),
            P("chain"),
        ),
        out_specs=P("chain", None, "shard", None),
        check_vma=False,
    )
```

time: 186 us -> 117 us (0.63)
  the two profiles are of different devices: /device:TPU:99 before, /device:TPU:223 now
where the time goes in v1:
time: 117 us
  Pallas kernels  113 us (97%)
  local copies, waits for them, and re-layouts  3.13 us (3%)
  between operations  1.3 us (1%)
    pallas_call x1, Pallas kernels, body(): pl.pallas_call(functools.partial(kernel, workers), out_shape=jax.ShapeDty...  113 us
    unnamed x1, local copies, waits for them, and re-layouts  3.13 us

profile of v1, /device:TPU:223, one launch (start us, length us, event | category | flops | bytes accessed | tf_op | source)
XLA Modules:
  0.0 117.2 jit_solution(14145155957419970097)
XLA Ops:
  1.3 112.8 %shard_map.91 = bf16[1,2,128,4096]{3,2,1,0:T(8,128)(2,1)} custom-call(bf16[1,2,128,4096]{3,2,1,0:T(8,128)(2,1)} %w_pair.1, bf16[1,128,4096]{2,1,0:T(8,128)(2,1)} %w_down.1, bf16[1,256,4096]{2,1,0:T(8,128)(2,1)} %tokens.1, bf16[1,256,4096]{2,1,0:T(8,128)(2,1)} %cotangent.1, s32[1,256]{1,0:T(1,128)} %seq_ids.1, bf16[1,2,128,4096]{3,2,1,0:T(8,128)(2,1)} %msg_left.1, ...), custom_call_target="tpu_custom_call" | custom-call | tf_op jit(solution)/shard_map/pallas_call | solution.py:333
  114.1 3.1 %copy.13 = bf16[1,2,128,4096]{3,2,1,0:T(8,128)(2,1)} copy(bf16[1,2,128,4096]{3,2,1,0:T(8,128)(2,1)} %shard_map.91) | data formatting | bytes 4194304

commit v2 on v1

--- a/solution.py
+++ b/solution.py
@@ -15,6 +15,10 @@
 
 CHUNKS = ((0, 32), (32, 32), (64, 32), (96, 16), (112, 16))
 TILE = 512
+
+X, Z = 4, 8
+PIECE = 16
+RELAYS = 12
 
 
 def dot_nt(a, b):
@@ -66,9 +70,7 @@
     cnt_l_out,
     cnt_l,
     cnt_r,
-    new,
     load_sem,
-    out_sem,
     y_send,
     y_recv,
     wd_send,
@@ -79,6 +81,9 @@
     r_recv,
     l_send,
     l_recv,
+    relay_buf,
+    relay_send,
+    relay_recv,
 ):
     me, side = lax.axis_index("chain"), lax.axis_index("shard")
     partner = (me, 1 - side)
@@ -100,6 +105,23 @@
     def cols(j):
         return pl.ds(pl.multiple_of(j * TILE, TILE), TILE)
 
+    edge_r, edge_l = workers // 2 - 1, workers // 2
+    x, z, core, upper = (me // (2 * Z)) % X, (me // 2) % Z, me % 2, me >= edge_l
+
+    def relay_right(p):
+        return (edge_l + ((X - 1 - p % X) * Z + (Z - 1 + p // X) % Z) * 2 + 1, side)
+
+    def relay_left(p):
+        return (((p % X) * Z + (Z - p // X) % Z) * 2, side)
+
+    on_right = upper & (core == 1) & ((z + 1) % Z < RELAYS // X)
+    on_left = jnp.logical_not(upper) & (core == 0) & ((Z - z) % Z < RELAYS // X)
+    piece = jnp.where(upper, (z + 1) % Z * X + X - 1 - x, (Z - z) % Z * X + x)
+    piece = jnp.where(on_right | on_left, piece, 0)
+    piece_rows = pl.ds(pl.multiple_of(piece // 2 * PIECE, PIECE), PIECE)
+    piece_chunk = sum((piece // 2 * PIECE >= r0).astype(jnp.int32) for r0, _ in CHUNKS) - 1
+    relayed = [r0 + r <= RELAYS // 2 * PIECE for r0, r in CHUNKS] + [False]
+
     barrier = pltpu.get_barrier_semaphore()
     pl.semaphore_signal(barrier, inc=1, device_id=partner, device_id_type=MESH)
 
@@ -110,6 +132,24 @@
     @pl.when(has_right)
     def _():
         pl.semaphore_signal(barrier, inc=1, device_id=right, device_id_type=MESH)
+
+    @pl.when(on_right)
+    def _():
+        pl.semaphore_signal(barrier, inc=1, device_id=(edge_r, side), device_id_type=MESH)
+
+    @pl.when(on_left)
+    def _():
+        pl.semaphore_signal(barrier, inc=1, device_id=(edge_l, side), device_id_type=MESH)
+
+    @pl.when(me == edge_l)
+    def _():
+        for p in range(RELAYS):
+            pl.semaphore_signal(barrier, inc=1, device_id=relay_right(p), device_id_type=MESH)
+
+    @pl.when(me == edge_r)
+    def _():
+        for p in range(RELAYS):
+            pl.semaphore_signal(barrier, inc=1, device_id=relay_left(p), device_id_type=MESH)
 
     loads = [
         pltpu.make_async_copy(src, dst, load_sem.at[k])
@@ -130,7 +170,10 @@
     for load in loads:
         load.start()
 
-    pl.semaphore_wait(barrier, 1 + has_left.astype(jnp.int32) + has_right.astype(jnp.int32))
+    greeted = 1 + has_left.astype(jnp.int32) + has_right.astype(jnp.int32)
+    greeted += (on_right | on_left).astype(jnp.int32)
+    greeted += RELAYS * ((me == edge_l) | (me == edge_r)).astype(jnp.int32)
+    pl.semaphore_wait(barrier, greeted)
 
     ids_copy = remote(seq_ids, ids_p, y_send.at[0], y_recv.at[0], partner)
     tok_copy = remote(tokens.at[0], tok_p, y_send.at[1], y_recv.at[1], partner)
@@ -156,21 +199,53 @@
         )
         for c, (r0, r) in enumerate(CHUNKS)
     ] + [remote(cnt_l_out, cnt_r, l_send.at[n], l_recv.at[n], left)]
-    out_copies = [
-        pltpu.make_async_copy(
-            new.at[:, pl.ds(r0, r)], out.at[0, :, pl.ds(r0, r)], out_sem.at[c]
-        )
-        for c, (r0, r) in enumerate(CHUNKS)
-    ]
+    to_left = remote(
+        relay_buf, recv_l.at[piece % 2, piece_rows], relay_send, r_recv.at[piece_chunk], (edge_l, side)
+    )
+    to_right = remote(
+        relay_buf, recv_r.at[piece % 2, piece_rows], relay_send, l_recv.at[piece_chunk], (edge_r, side)
+    )
+
+    arrival = remote(relay_buf, relay_buf, relay_send, relay_recv, (edge_l, side))
+
+    def send_pieces(c, source, send, relay):
+        r0, r = CHUNKS[c]
+        for p in range(r0 // PIECE * 2, (r0 + r) // PIECE * 2):
+            remote(
+                source.at[p % 2, pl.ds(p // 2 * PIECE, PIECE)], relay_buf, send.at[c], relay_recv, relay(p)
+            ).start()
 
     def send_chain(c):
-        @pl.when(has_right)
+        @pl.when((has_right & (me != edge_r)) if relayed[c] else has_right)
         def _():
             r_copies[c].start()
 
-        @pl.when(has_left)
+        @pl.when((has_left & (me != edge_l)) if relayed[c] else has_left)
         def _():
             l_copies[c].start()
+
+        if relayed[c]:
+
+            @pl.when(me == edge_r)
+            def _():
+                send_pieces(c, send_r, r_send, relay_right)
+
+            @pl.when(me == edge_l)
+            def _():
+                send_pieces(c, send_l, l_send, relay_left)
+
+    def forward(c):
+        if c >= 0 and relayed[c]:
+
+            @pl.when(on_right & (piece_chunk == c))
+            def _():
+                arrival.wait_recv()
+                to_left.start()
+
+            @pl.when(on_left & (piece_chunk == c))
+            def _():
+                arrival.wait_recv()
+                to_right.start()
 
     ids_copy.start()
     wd_copies[0].start()
@@ -247,6 +322,7 @@
 
         lax.fori_loop(0, tiles, tile, 0)
         send_chain(c)
+        forward(c - 1)
 
     partner_grad_hidden(0)
     for c in range(1, min(3, n)):
@@ -297,11 +373,10 @@
                 + recv_l[:, r0 : r0 + r, cols(j)].astype(F32)
                 + recv_r[:, r0 : r0 + r, cols(j)].astype(F32)
             )
-            new[:, r0 : r0 + r, cols(j)] = (total * inverse.reshape(1, 1, TILE)).astype(BF16)
+            out[0, :, r0 : r0 + r, cols(j)] = (total * inverse.reshape(1, 1, TILE)).astype(BF16)
             return carry
 
         lax.fori_loop(0, tiles, tile, 0)
-        out_copies[c].start()
 
     ids_copy.wait_send()
     tok_copy.wait_send()
@@ -318,8 +393,13 @@
         def _(c=c):
             l_copies[c].wait_send()
 
-    for copy in out_copies:
-        copy.wait()
+    @pl.when(on_right)
+    def _():
+        to_left.wait_send()
+
+    @pl.when(on_left)
+    def _():
+        to_right.wait_send()
 
 
 def body(w_pair, w_down, tokens, cotangent, seq_ids, msg_left, msg_right, count_left, count_right):
@@ -332,9 +412,9 @@
     vm, dma = pltpu.VMEM, pltpu.SemaphoreType.DMA
     return pl.pallas_call(
         functools.partial(kernel, workers),
-        out_shape=jax.ShapeDtypeStruct(w_pair.shape, BF16),
+        out_shape=pltpu.VMEM(w_pair.shape, BF16),
         in_specs=[any_space] * 9,
-        out_specs=any_space,
+        out_specs=pl.BlockSpec(memory_space=pltpu.VMEM),
         scratch_shapes=[
             vm(pair, BF16),
             vm((hidden, width), BF16),
@@ -363,9 +443,7 @@
             vm((1, TILE), jnp.int32),
             vm((1, TILE), jnp.int32),
             vm((1, TILE), jnp.int32),
-            vm(pair, BF16),
             dma((9,)),
-            dma((n,)),
             dma((2,)),
             dma((2,)),
             dma((n,)),
@@ -376,9 +454,12 @@
             dma((n + 1,)),
             dma((n + 1,)),
             dma((n + 1,)),
+            vm((PIECE, width), BF16),
+            dma(()),
+            dma(()),
         ],
         compiler_params=pltpu.CompilerParams(
-            collective_id=0, has_side_effects=True, vmem_limit_bytes=60 * 1024 * 1024
+            collective_id=0, has_side_effects=True, vmem_limit_bytes=61 * 1024 * 1024
         ),
     )(w_pair, w_down, tokens, cotangent, seq_ids, msg_left, msg_right, count_left, count_right)
 

time: 117 us -> 103 us (0.88)
  the two profiles are of different devices: /device:TPU:223 before, /device:TPU:24 now
where the time goes in v2:
time: 103 us; the launch traced here: 102 us
  Pallas kernels  99.8 us (97%)
  local copies, waits for them, and re-layouts  1.32 us (1%)
  between operations  1.3 us (1%)
    pallas_call x1, Pallas kernels, body(): pl.pallas_call(functools.partial(kernel, workers), out_shape=pltpu.VMEM(w...  99.8 us

profile of v2, /device:TPU:24, one launch (start us, length us, event | category | flops | bytes accessed | tf_op | source)
XLA Modules:
  0.0 102.4 jit_solution(10336684513242379519)
XLA Ops:
  1.3 99.8 %shard_map.91 = bf16[1,2,128,4096]{3,2,1,0:T(8,128)(2,1)S(1)} custom-call(bf16[1,2,128,4096]{3,2,1,0:T(8,128)(2,1)} %w_pair.1, bf16[1,128,4096]{2,1,0:T(8,128)(2,1)} %w_down.1, bf16[1,256,4096]{2,1,0:T(8,128)(2,1)} %tokens.1, bf16[1,256,4096]{2,1,0:T(8,128)(2,1)} %cotangent.1, s32[1,256]{1,0:T(1,128)} %seq_ids.1, bf16[1,2,128,4096]{3,2,1,0:T(8,128)(2,1)} %msg_left.1, ...), custom_call_target="tpu_custom_call" | custom-call | tf_op jit(solution)/shard_map/pallas_call | solution.py:413
  101.1 1.3 %copy.11 = bf16[1,2,128,4096]{3,2,1,0:T(8,128)(2,1)} copy(bf16[1,2,128,4096]{3,2,1,0:T(8,128)(2,1)S(1)} %shard_map.91) | data formatting | bytes 4194304

commit v3 on v1

--- a/solution.py
+++ b/solution.py
@@ -13,8 +13,11 @@
 learn_rate = 1.0
 SEQS = 8
 
-CHUNKS = ((0, 32), (32, 32), (64, 32), (96, 16), (112, 16))
-TILE = 512
+CHUNKS = tuple((r, 16) for r in range(0, 128, 16))
+TILE = 1024
+
+PIECE, CUTS = 16, 4
+RELAYS = 24
 
 
 def dot_nt(a, b):
@@ -66,9 +69,7 @@
     cnt_l_out,
     cnt_l,
     cnt_r,
-    new,
     load_sem,
-    out_sem,
     y_send,
     y_recv,
     wd_send,
@@ -79,6 +80,9 @@
     r_recv,
     l_send,
     l_recv,
+    relay_buf,
+    relay_send,
+    relay_recv,
 ):
     me, side = lax.axis_index("chain"), lax.axis_index("shard")
     partner = (me, 1 - side)
@@ -100,6 +104,22 @@
     def cols(j):
         return pl.ds(pl.multiple_of(j * TILE, TILE), TILE)
 
+    core, upper = me % 2, me >= workers // 2
+    column = jnp.where(upper, last - me, me) // 2
+    is_edge = column == 0
+    is_relay = (column >= 1) & (column <= RELAYS)
+    edge = jnp.where(upper, last - 1 + core, core)
+    piece = jnp.where(is_relay, column - 1, 0)
+
+    def relay(p):
+        return jnp.where(upper, edge - 2 * (p + 1), edge + 2 * (p + 1))
+
+    def piece_of(p):
+        first, start = p // CUTS * PIECE, p % CUTS * (width // CUTS)
+        if not isinstance(p, int):
+            first, start = pl.multiple_of(first, PIECE), pl.multiple_of(start, width // CUTS)
+        return pl.ds(first, PIECE), pl.ds(start, width // CUTS)
+
     barrier = pltpu.get_barrier_semaphore()
     pl.semaphore_signal(barrier, inc=1, device_id=partner, device_id_type=MESH)
 
@@ -110,6 +130,10 @@
     @pl.when(has_right)
     def _():
         pl.semaphore_signal(barrier, inc=1, device_id=right, device_id_type=MESH)
+
+    @pl.when(is_relay)
+    def _():
+        pl.semaphore_signal(barrier, inc=1, device_id=(edge, 1 - side), device_id_type=MESH)
 
     loads = [
         pltpu.make_async_copy(src, dst, load_sem.at[k])
@@ -130,7 +154,9 @@
     for load in loads:
         load.start()
 
-    pl.semaphore_wait(barrier, 1 + has_left.astype(jnp.int32) + has_right.astype(jnp.int32))
+    greeted = 1 + has_left.astype(jnp.int32) + has_right.astype(jnp.int32)
+    greeted += RELAYS * is_edge.astype(jnp.int32)
+    pl.semaphore_wait(barrier, greeted)
 
     ids_copy = remote(seq_ids, ids_p, y_send.at[0], y_recv.at[0], partner)
     tok_copy = remote(tokens.at[0], tok_p, y_send.at[1], y_recv.at[1], partner)
@@ -156,12 +182,10 @@
         )
         for c, (r0, r) in enumerate(CHUNKS)
     ] + [remote(cnt_l_out, cnt_r, l_send.at[n], l_recv.at[n], left)]
-    out_copies = [
-        pltpu.make_async_copy(
-            new.at[:, pl.ds(r0, r)], out.at[0, :, pl.ds(r0, r)], out_sem.at[c]
-        )
-        for c, (r0, r) in enumerate(CHUNKS)
-    ]
+    taken = RELAYS // CUTS * PIECE
+    rest = pl.ds(taken, rows - taken)
+    rest_copy = remote(tokens.at[0, rest], tok_p.at[rest], y_send.at[1], y_recv.at[1], partner)
+    handed = remote(relay_buf, tok_p.at[piece_of(piece)], relay_send, y_recv.at[1], (edge, side))
 
     def send_chain(c):
         @pl.when(has_right)
@@ -174,7 +198,19 @@
 
     ids_copy.start()
     wd_copies[0].start()
-    tok_copy.start()
+
+    @pl.when(jnp.logical_not(is_edge))
+    def _():
+        tok_copy.start()
+
+    @pl.when(is_edge)
+    def _():
+        rest_copy.start()
+        for p in range(RELAYS):
+            at = piece_of(p)
+            remote(
+                tokens.at[(0, *at)], relay_buf, y_send.at[1], relay_recv, (relay(p), 1 - side)
+            ).start()
 
     @pl.when(jnp.logical_not(has_left))
     def _():
@@ -249,6 +285,12 @@
         send_chain(c)
 
     partner_grad_hidden(0)
+
+    @pl.when(is_relay)
+    def _():
+        remote(relay_buf, relay_buf, relay_send, relay_recv, (edge, side)).wait_recv()
+        handed.start()
+
     for c in range(1, min(3, n)):
         wd_copies[c].start()
 
@@ -297,11 +339,10 @@
                 + recv_l[:, r0 : r0 + r, cols(j)].astype(F32)
                 + recv_r[:, r0 : r0 + r, cols(j)].astype(F32)
             )
-            new[:, r0 : r0 + r, cols(j)] = (total * inverse.reshape(1, 1, TILE)).astype(BF16)
+            out[0, :, r0 : r0 + r, cols(j)] = (total * inverse.reshape(1, 1, TILE)).astype(BF16)
             return carry
 
         lax.fori_loop(0, tiles, tile, 0)
-        out_copies[c].start()
 
     ids_copy.wait_send()
     tok_copy.wait_send()
@@ -318,8 +359,9 @@
         def _(c=c):
             l_copies[c].wait_send()
 
-    for copy in out_copies:
-        copy.wait()
+    @pl.when(is_relay)
+    def _():
+        handed.wait_send()
 
 
 def body(w_pair, w_down, tokens, cotangent, seq_ids, msg_left, msg_right, count_left, count_right):
@@ -332,9 +374,9 @@
     vm, dma = pltpu.VMEM, pltpu.SemaphoreType.DMA
     return pl.pallas_call(
         functools.partial(kernel, workers),
-        out_shape=jax.ShapeDtypeStruct(w_pair.shape, BF16),
+        out_shape=pltpu.VMEM(w_pair.shape, BF16),
         in_specs=[any_space] * 9,
-        out_specs=any_space,
+        out_specs=pl.BlockSpec(memory_space=pltpu.VMEM),
         scratch_shapes=[
             vm(pair, BF16),
             vm((hidden, width), BF16),
@@ -363,9 +405,7 @@
             vm((1, TILE), jnp.int32),
             vm((1, TILE), jnp.int32),
             vm((1, TILE), jnp.int32),
-            vm(pair, BF16),
             dma((9,)),
-            dma((n,)),
             dma((2,)),
             dma((2,)),
             dma((n,)),
@@ -376,9 +416,12 @@
             dma((n + 1,)),
             dma((n + 1,)),
             dma((n + 1,)),
+            vm((PIECE, width // CUTS), BF16),
+            dma(()),
+            dma(()),
         ],
         compiler_params=pltpu.CompilerParams(
-            collective_id=0, has_side_effects=True, vmem_limit_bytes=60 * 1024 * 1024
+            collective_id=0, has_side_effects=True, vmem_limit_bytes=61 * 1024 * 1024
         ),
     )(w_pair, w_down, tokens, cotangent, seq_ids, msg_left, msg_right, count_left, count_right)
 

time: 117 us -> 93.9 us (0.80)
  the two profiles are of different devices: /device:TPU:223 before, /device:TPU:99 now
where the time goes in v3:
time: 93.9 us; the launch traced here: 93.8 us
  Pallas kernels  91.2 us (97%)
  local copies, waits for them, and re-layouts  1.32 us (1%)
  between operations  1.3 us (1%)
    pallas_call x1, Pallas kernels, body(): pl.pallas_call(functools.partial(kernel, workers), out_shape=pltpu.VMEM(w...  91.2 us

profile of v3, /device:TPU:99, one launch (start us, length us, event | category | flops | bytes accessed | tf_op | source)
XLA Modules:
  0.0 93.8 jit_solution(8030859999049695354)
XLA Ops:
  1.3 91.2 %shard_map.91 = bf16[1,2,128,4096]{3,2,1,0:T(8,128)(2,1)S(1)} custom-call(bf16[1,2,128,4096]{3,2,1,0:T(8,128)(2,1)} %w_pair.1, bf16[1,128,4096]{2,1,0:T(8,128)(2,1)} %w_down.1, bf16[1,256,4096]{2,1,0:T(8,128)(2,1)} %tokens.1, bf16[1,256,4096]{2,1,0:T(8,128)(2,1)} %cotangent.1, s32[1,256]{1,0:T(1,128)} %seq_ids.1, bf16[1,2,128,4096]{3,2,1,0:T(8,128)(2,1)} %msg_left.1, ...), custom_call_target="tpu_custom_call" | custom-call | tf_op jit(solution)/shard_map/pallas_call | solution.py:375
  92.5 1.3 %copy.11 = bf16[1,2,128,4096]{3,2,1,0:T(8,128)(2,1)} copy(bf16[1,2,128,4096]{3,2,1,0:T(8,128)(2,1)S(1)} %shard_map.91) | data formatting | bytes 4194304
